TPU v7x, 32 devices: a whole 2x2x4 slice. The times are simulated.
32 devices in a mesh: dp: 8 (over y, x, core), branch: 4 (over z).
Axes of the slice: x: 2, y: 2, z: 4, core: 2. Of those that a mesh axis runs over, the one named last changes fastest.
Arguments:
- image_hidden: bfloat16 [4096, 1024], P('dp', 'branch'), may hold values from -8 to 8
- text_hidden: bfloat16 [4096, 768], P('dp', 'branch'), may hold values from -8 to 8
- image_proj: bfloat16 [1024, 768], replicated, may hold values from -0.1875 to 0.1875
- text_proj: bfloat16 [768, 768], replicated, may hold values from -0.21650635 to 0.21650635
- log_inverse_sharpness: float32 [1], replicated, may hold values from 4 to 5.9
- partner: int32 [4096], replicated, may hold values from 0 to 4095, each once
Outputs:
- loss: float32 [1], replicated
- grad_log_scale: float32 [1], replicated
- grad_image_hidden: bfloat16 [4096, 1024], P('dp', 'branch')
- grad_text_hidden: bfloat16 [4096, 768], P('dp', 'branch')
- grad_image_proj: float32 [1024, 768], P('branch')
- grad_text_proj: float32 [768, 768], P('branch')
Inputs may be any that keep to these rules, and one draw needn't show every extreme that they name: `partner`: each text index appears exactly once.
All inputs are finite; a program needn't handle non-finite values.
Results may differ from a plain program's by a relative error of at most 0.0029.
The roundings to bfloat16 on the way count: a program that leaves them out, or rounds other values in their place, can miss the bound.
Values may be sent and summed in bfloat16 or wider, within the bound.
A program may use at most 64 MiB of HBM per device.

v0:
```python
import jax
import jax.numpy as jnp
from jax import lax
from jax.sharding import PartitionSpec as P

NORM_EPSILON = 1e-06


def normalize(raw_rows):
    lengths = jnp.sqrt(jnp.sum(raw_rows * raw_rows, axis=1, keepdims=True) + NORM_EPSILON)
    unit_rows = raw_rows / lengths
    return (unit_rows, lengths, unit_rows.astype(jnp.bfloat16))


def unnormalize(upstream, unit_rows, lengths):
    radial = jnp.sum(upstream * unit_rows, axis=1, keepdims=True)
    return ((upstream - unit_rows * radial) / lengths).astype(jnp.bfloat16)


def per_device(image_hidden, text_hidden, image_proj, text_proj, log_inverse_sharpness, partner):
    branch_count = lax.axis_size("branch")
    data_count = lax.axis_size("dp")
    branch_pos = lax.axis_index("branch")
    data_pos = lax.axis_index("dp")
    group_rows = image_hidden.shape[0]
    own_rows = group_rows // branch_count
    image_cols = image_hidden.shape[1]
    text_cols = text_hidden.shape[1]
    image_slab = lax.dynamic_slice_in_dim(image_proj, branch_pos * image_cols, image_cols, 0)
    text_slab = lax.dynamic_slice_in_dim(text_proj, branch_pos * text_cols, text_cols, 0)
    image_local, text_local = (
        lax.all_to_all(image_hidden, "branch", split_axis=0, concat_axis=1, tiled=True),
        lax.all_to_all(text_hidden, "branch", split_axis=0, concat_axis=1, tiled=True),
    )
    image_raw = jnp.dot(image_local, image_proj, preferred_element_type=jnp.float32)
    text_raw = jnp.dot(text_local, text_proj, preferred_element_type=jnp.float32)
    image_unit, image_length, image_emb = normalize(image_raw)
    text_unit, text_length, caption_feature_entries = normalize(text_raw)
    normalized_exponent_divisor = jnp.exp(log_inverse_sharpness[0])
    column_count = own_rows * data_count
    total_pairs = group_rows * data_count
    denominator = 2.0 * total_pairs
    group_emb = lax.all_gather(image_emb, "branch", axis=0, tiled=True)
    row_partner = lax.dynamic_slice_in_dim(partner, data_pos * group_rows, group_rows, 0)

    def column_ident(positions):
        return (positions // own_rows * branch_count + branch_pos) * own_rows + positions % own_rows

    block_piece = lax.all_gather(caption_feature_entries, "dp", axis=0, tiled=True)
    row_peak = jnp.full((group_rows,), -jnp.inf, jnp.float32)
    row_mass = jnp.zeros((group_rows,), jnp.float32)
    piece_width = block_piece.shape[0]
    matching_cosine_scores = normalized_exponent_divisor * lax.dot_general(
        group_emb, block_piece, (((1,), (1,)), ((), ())), preferred_element_type=jnp.float32
    )
    logits_kept = matching_cosine_scores
    column_ids = column_ident(jnp.arange(piece_width, dtype=jnp.int32))
    matched = row_partner[:, None] == column_ids[None, :]
    positive = jnp.sum(jnp.where(matched, matching_cosine_scores, 0.0), axis=1)
    new_peak = jnp.max(matching_cosine_scores, axis=1)
    row_mass = row_mass * jnp.exp(row_peak - new_peak) + jnp.sum(
        jnp.exp(matching_cosine_scores - new_peak[:, None]), axis=1
    )
    piece_peak = jnp.max(matching_cosine_scores, axis=0)
    piece_mass = jnp.sum(jnp.exp(matching_cosine_scores - piece_peak[None, :]), axis=0)
    column_peak = piece_peak
    column_mass = piece_mass
    (
        retained_text_rows,
        matching_cosine_scores,
        row_peak,
        row_mass,
        positive,
        column_peak,
        column_mass,
    ) = (block_piece, logits_kept, new_peak, row_mass, positive, column_peak, column_mass)
    row_highest = lax.pmax(row_peak, "branch")
    row_mass, positive = lax.psum((row_mass * jnp.exp(row_peak - row_highest), positive), "branch")
    row_peak = row_highest
    column_highest = lax.pmax(column_peak, "dp")
    column_mass = lax.psum(column_mass * jnp.exp(column_peak - column_highest), "dp")
    column_peak = column_highest
    row_lse = row_peak + jnp.log(row_mass)
    col_lse = column_peak + jnp.log(column_mass)
    column_ids = column_ident(jnp.arange(column_count, dtype=jnp.int32))
    matched = (row_partner[:, None] == column_ids[None, :]).astype(jnp.float32)
    weights = (
        jnp.exp(matching_cosine_scores - row_lse[:, None])
        + jnp.exp(matching_cosine_scores - col_lse[None, :])
        - 2.0 * matched
    ) / denominator
    scale_part = jnp.sum(weights * matching_cosine_scores)
    reduced_width_parameters = weights.astype(jnp.bfloat16)
    picture_projection_matrix = lax.psum_scatter(
        normalized_exponent_divisor
        * jnp.dot(reduced_width_parameters, retained_text_rows, preferred_element_type=jnp.float32),
        "branch",
        scatter_dimension=0,
        tiled=True,
    )
    text_up = lax.psum_scatter(
        normalized_exponent_divisor
        * lax.dot_general(
            reduced_width_parameters,
            group_emb,
            (((0,), (0,)), ((), ())),
            preferred_element_type=jnp.float32,
        ),
        "dp",
        scatter_dimension=0,
        tiled=True,
    )
    image_down = unnormalize(picture_projection_matrix, image_unit, image_length)
    text_down = unnormalize(text_up, text_unit, text_length)
    image_gathered, text_gathered = (
        lax.all_gather(image_down, "branch", axis=0, tiled=True),
        lax.all_gather(text_down, "branch", axis=0, tiled=True),
    )
    grad_image_hidden = jnp.dot(
        image_gathered, image_slab.T, preferred_element_type=jnp.float32
    ).astype(jnp.bfloat16)
    grad_text_hidden = jnp.dot(
        text_gathered, text_slab.T, preferred_element_type=jnp.float32
    ).astype(jnp.bfloat16)
    image_weight = lax.dot_general(
        image_hidden, image_gathered, (((0,), (0,)), ((), ())), preferred_element_type=jnp.float32
    )
    text_weight = lax.dot_general(
        text_hidden, text_gathered, (((0,), (0,)), ((), ())), preferred_element_type=jnp.float32
    )
    grad_image_proj, grad_text_proj = lax.psum((image_weight, text_weight), "dp")
    own_row_terms = lax.dynamic_slice_in_dim(
        row_lse - 2.0 * positive, branch_pos * own_rows, own_rows, 0
    )
    own_col_terms = lax.dynamic_slice_in_dim(col_lse, data_pos * own_rows, own_rows, 0)
    loss_part = (jnp.sum(own_row_terms) + jnp.sum(own_col_terms)) / denominator
    loss_total, scale_total = lax.psum((loss_part, scale_part), ("dp", "branch"))
    return (
        loss_total.reshape(1),
        scale_total.reshape(1),
        grad_image_hidden,
        grad_text_hidden,
        grad_image_proj,
        grad_text_proj,
    )


def solution(mesh):
    placed = (P("dp", "branch"), P("dp", "branch"), P(), P(), P(), P())
    return jax.shard_map(
        per_device,
        mesh=mesh,
        in_specs=placed,
        out_specs=(
            P(),
            P(),
            P("dp", "branch"),
            P("dp", "branch"),
            P("branch", None),
            P("branch", None),
        ),
        check_vma=False,
    )
```

profile of v0, /device:TPU:0, one launch (start us, length us, event | category | flops | bytes accessed | tf_op | source)
XLA Modules:
  0.0 283.1 jit_solution(11487178637805667783)
XLA Ops:
  7.2 1.1 copy_bitcast_fusion
  8.3 13.6 %all_to_all.38 = bf16[4,128,192]{1,2,0:T(8,128)(2,1)S(1)} all-to-all(bf16[4,128,192]{1,2,0:T(8,128)(2,1)S(1)} %copy_bitcast_fusion), channel_id=1, replica_groups=mesh['dp'=8,'branch'=4] {'branch'}, dimensions={0} | all-to-all | bytes 393216 | tf_op jit(solution)/shard_map/all_to_all | solution.py:33
  21.9 1.7 multiply_reduce_fusion.3
  24.5 3.4 %all-to-all-start = ((bf16[4,128,256]{2,1,0:T(8,128)(2,1)}), bf16[4,128,256]{2,1,0:T(8,128)(2,1)S(1)}, u32[]{:S(2)}, u32[]{:S(2)}) async-start(bf16[4,128,256]{2,1,0:T(8,128)(2,1)} %bitcast.1), calls=%async_computation | async-start | bytes 524288 | tf_op jit(solution)/shard_map/all_to_all | solution.py:32
  29.4 6.6 %all-to-all-done = bf16[4,128,256]{2,1,0:T(8,128)(2,1)S(1)} async-done(((bf16[4,128,256]{2,1,0:T(8,128)(2,1)}), bf16[4,128,256]{2,1,0:T(8,128)(2,1)S(1)}, u32[]{:S(2)}, u32[]{:S(2)}) %all-to-all-start) | async-done | bytes 262176 | tf_op jit(solution)/shard_map/all_to_all | solution.py:32
  36.8 17.6 %all_gather.12 = bf16[512,768]{1,0:T(8,128)(2,1)S(1)} all-gather(bf16[128,768]{1,0:T(8,128)(2,1)S(1)} %fusion.19), channel_id=1, replica_groups=mesh['dp'=8,'branch'=4] {'branch'}, dimensions={0}, use_global_device_ids=true | all-gather | bytes 983040 | tf_op jit(solution)/shard_map/all_gather | solution.py:43
  54.4 3.8 %fusion.23 = (f32[1024]{0:T(1024)S(1)}, f32[512]{0:T(512)S(1)}, f32[512,1024]{1,0:T(8,128)}) fusion(bf16[512,768]{1,0:T(8,128)(2,1)S(1)} %all_gather.12, bf16[1024,768]{1,0:T(8,128)(2,1)} %all-gather.2.cloned.1.call-done, f32[]{:T(128)} %bitcast), kind=kOutput, calls=%fused_computation.55 | convolution fusion | flops 806877696 | bytes 4462596 | tf_op jit(solution)/shard_map/dot_general | solution.py:53
  58.2 10.3 %pmax.14 = f32[512]{0:T(512)S(1)} all-reduce(f32[512]{0:T(512)S(1)} %get-tuple-element.35), channel_id=1, replica_groups=mesh['dp'=8,'branch'=4] {'branch'}, use_global_device_ids=true, to_apply=%region_3.4 | all-reduce | flops 512 | bytes 4096 | tf_op jit(solution)/shard_map/pmax | solution.py:77
  68.5 11.8 %pmax.15 = f32[1024]{0:T(1024)S(1)} all-reduce(f32[1024]{0:T(1024)S(1)} %get-tuple-element.34), channel_id=1, replica_groups=mesh['dp'=8,'branch'=4] {'dp'}, use_global_device_ids=true, to_apply=%region_10.11 | all-reduce | flops 1024 | bytes 8192 | tf_op jit(solution)/shard_map/pmax | solution.py:80
  80.3 2.3 exponential_reduce_fusion
  82.7 11.9 %psum.51 = f32[1024]{0:T(1024)S(1)} all-reduce(f32[1024]{0:T(1024)S(1)} %exponential_multiply_fusion), channel_id=1, replica_groups=mesh['dp'=8,'branch'=4] {'dp'}, use_global_device_ids=true, to_apply=%region_12.13 | all-reduce | flops 1024 | bytes 8192 | tf_op jit(solution)/shard_map/psum | solution.py:81
  94.6 8.4 %psum.49 = f32[512]{0:T(512)S(1)} all-reduce(f32[512]{0:T(512)S(1)} %exponential_multiply_fusion.1), channel_id=1, replica_groups=mesh['dp'=8,'branch'=4] {'branch'}, use_global_device_ids=true, to_apply=%region_5.6 | all-reduce | flops 512 | bytes 4096 | tf_op jit(solution)/shard_map/psum | solution.py:78
  103.0 4.8 %convolution_multiply_fusion.2 = f32[512,768]{1,0:T(8,128)} fusion(bf16[1024,768]{1,0:T(8,128)(2,1)} %all-gather.2.cloned.1.call-done, f32[]{:T(128)} %bitcast, f32[512,1024]{1,0:T(8,128)} %get-tuple-element.44, f32[1024]{0:T(1024)S(1)} %log_add_fusion, f32[512]{0:T(512)S(1)} %log_add_fusion.1, s32[1024]{0:T(1024)S(1)} %fusion.15, s32[512]{0:T(512)S(1)} %dynamic_slice.15), kind=kOutput, calls=%fused_computation.11 | convolution fusion | flops 809893888 | bytes 5255172 | tf_op jit(solution)/shard_map/dot_general | solution.py:96
  107.9 4.8 %convolution_multiply_fusion = f32[1024,768]{1,0:T(8,128)} fusion(bf16[512,768]{1,0:T(8,128)(2,1)S(1)} %all_gather.12, f32[]{:T(128)} %bitcast, f32[512,1024]{1,0:T(8,128)} %get-tuple-element.44, f32[1024]{0:T(1024)S(1)} %log_add_fusion, f32[512]{0:T(512)S(1)} %log_add_fusion.1, s32[1024]{0:T(1024)S(1)} %fusion.15, s32[512]{0:T(512)S(1)} %dynamic_slice.15), kind=kOutput, calls=%fused_computation.9 | convolution fusion | flops 810287104 | bytes 6041604 | tf_op jit(solution)/shard_map/dot_general | solution.py:103
  113.5 3.6 %multiply_reduce_fusion = (f32[]{:T(128)}, f32[512]{0:T(512)S(1)}) fusion(f32[512,1024]{1,0:T(8,128)} %get-tuple-element.44, f32[1024]{0:T(1024)S(1)} %log_add_fusion, f32[512]{0:T(512)S(1)} %log_add_fusion.1, s32[1024]{0:T(1024)S(1)} %fusion.15, s32[512]{0:T(512)S(1)} %dynamic_slice.15), kind=kLoop, calls=%fused_computation.5 | loop fusion | flops 5766655 | bytes 2111492 | tf_op jit(solution)/shard_map/reduce_sum | solution.py:92
  117.1 11.2 %psum.50 = f32[512]{0:T(512)S(1)} all-reduce(f32[512]{0:T(512)S(1)} %get-tuple-element.31), channel_id=1, replica_groups=mesh['dp'=8,'branch'=4] {'branch'}, use_global_device_ids=true, to_apply=%region_7.8 | all-reduce | flops 512 | bytes 4096 | tf_op jit(solution)/shard_map/psum | solution.py:78
  128.3 14.0 %reduce-scatter.3.cloned.1.call-done = f32[128,768]{1,0:T(8,128)} async-done(((f32[512,768]{1,0:T(8,128)}), f32[128,768]{1,0:T(8,128)}) %reduce-scatter.3.cloned.1.call-update) | async-done | bytes 393232 | tf_op jit(solution)/shard_map/reduce_scatter | solution.py:94
  142.3 1.2 multiply_reduce_fusion.2
  143.5 1.1 divide_convert_fusion.1
  144.6 17.9 %all_gather.14 = bf16[512,768]{1,0:T(8,128)(2,1)S(1)} all-gather(bf16[128,768]{1,0:T(8,128)(2,1)S(1)} %divide_convert_fusion.1), channel_id=1, replica_groups=mesh['dp'=8,'branch'=4] {'branch'}, dimensions={0}, use_global_device_ids=true | all-gather | bytes 983040 | tf_op jit(solution)/shard_map/all_gather | solution.py:116
  162.5 2.2 convolution_bitcast_fusion
  164.8 25.9 %reduce-scatter.5.cloned.1.call-done = f32[128,768]{1,0:T(8,128)} async-done(((f32[1024,768]{1,0:T(8,128)}), f32[128,768]{1,0:T(8,128)}) %reduce-scatter.5.cloned.1.call-update) | async-done | bytes 393232 | tf_op jit(solution)/shard_map/reduce_scatter | solution.py:101
  190.7 1.2 multiply_reduce_fusion.1
  191.8 1.1 divide_convert_fusion
  193.0 19.6 %all_gather.15 = bf16[512,768]{1,0:T(8,128)(2,1)S(1)} all-gather(bf16[128,768]{1,0:T(8,128)(2,1)S(1)} %divide_convert_fusion), channel_id=1, replica_groups=mesh['dp'=8,'branch'=4] {'branch'}, dimensions={0}, use_global_device_ids=true | all-gather | bytes 983040 | tf_op jit(solution)/shard_map/all_gather | solution.py:117
  212.5 2.1 convolution_bitcast_fusion.1
  216.6 38.5 %all-reduce = (f32[1]{0:T(128)}, f32[1]{0:T(128)}) all-reduce(f32[1]{0:T(128)} %bitcast.6, f32[1]{0:T(128)} %bitcast.7), channel_id=1, replica_groups=mesh['dp'=8,'branch'=4] {'dp','branch'}, use_global_device_ids=true, to_apply=%region_14.15 | all-reduce | flops 2 | bytes 16 | tf_op jit(solution)/shard_map/psum | solution.py:137
  255.1 1.1 convolution_convert_fusion
  256.2 2.0 convolution_convert_fusion.1
  258.3 14.1 %all-reduce.4.cloned.1.call-done = (f32[256,768]{0,1:T(8,128)}, f32[192,768]{1,0:T(8,128)}) async-done(((f32[256,768]{0,1:T(8,128)}, f32[192,768]{1,0:T(8,128)}), (f32[256,768]{0,1:T(8,128)}, f32[192,768]{1,0:T(8,128)})) %all-reduce.4.cloned.1.call-update) | async-done | bytes 1376272 | tf_op jit(solution)/shard_map/psum | solution.py:131
  272.3 2.3 copy.19
  274.6 1.9 copy.25
  (26 shorter events, 4.0 us)
Async XLA Ops:
  7.2 29.0 %copy-start = (bf16[1024,768]{1,0:T(8,128)(2,1)S(1)}, bf16[1024,768]{1,0:T(8,128)(2,1)}, u32[]{:S(2)}) copy-start(bf16[1024,768]{1,0:T(8,128)(2,1)} %param.8) | copy-start | bytes 4718596
  7.2 47.2 %all-gather.2.cloned.1.call-start = ((), (), s32[]{:S(2)}) async-start(), calls=%async_computation.4 | async-start | bytes 1769472 | tf_op jit(solution)/shard_map/all_gather | solution.py:49
  24.5 11.6 %all-to-all-start = ((bf16[4,128,256]{2,1,0:T(8,128)(2,1)}), bf16[4,128,256]{2,1,0:T(8,128)(2,1)S(1)}, u32[]{:S(2)}, u32[]{:S(2)}) async-start(bf16[4,128,256]{2,1,0:T(8,128)(2,1)} %bitcast.1), calls=%async_computation | async-start | bytes 524288 | tf_op jit(solution)/shard_map/all_to_all | solution.py:32
  27.9 114.4 %reduce-scatter.3.cloned.1.call-start = ((), (), s32[]{:S(2)}) async-start(), calls=%async_computation.5 | async-start | bytes 1966080 | tf_op jit(solution)/shard_map/reduce_scatter | solution.py:94
  107.8 82.8 %reduce-scatter.5.cloned.1.call-start = ((), (), s32[]{:S(2)}) async-start(), calls=%async_computation.6 | async-start | bytes 3538944 | tf_op jit(solution)/shard_map/reduce_scatter | solution.py:101
  112.8 159.6 %all-reduce.4.cloned.1.call-start = ((), (), s32[]{:S(2)}) async-start(), calls=%async_computation.7 | async-start | bytes 2752512 | tf_op jit(solution)/shard_map/psum | solution.py:131
Sparse Core Ops, SparseCore 0:
  24.6 24.6 all-gather.1
  108.0 34.2 reduce-scatter.2
  145.7 44.9 reduce-scatter.4
  214.8 57.5 all-reduce.3
where the time goes:
time: 284 us; the launch traced here: 283 us
  blocking collectives  161 us (57%)
  waiting for transfers between devices  60.6 us (21%)
  matrix products  23.1 us (8%)
  between operations  15.9 us (6%)
  other arithmetic  12.9 us (5%)
  local copies, waits for them, and re-layouts  6.21 us (2%)
  starting transfers between devices  3.58 us (1%)
    psum x1, blocking collectives, per_device(): lax.psum((loss_part, scale_part), ('dp', 'branch'))  38.5 us
    reduce_scatter x1, waiting for transfers between devices, per_device(): lax.psum_scatter(normalized_exponent_divisor * lax.dot_general(reduced_wi...  25.9 us
    all_gather x1, blocking collectives, per_device(): lax.all_gather(text_down, 'branch', axis=0, tiled=True)  19.6 us
    psum x2, blocking collectives, per_device(): lax.psum((row_mass * jnp.exp(row_peak - row_highest), positive), 'branch')  19.6 us
    all_gather x1, blocking collectives, per_device(): lax.all_gather(image_down, 'branch', axis=0, tiled=True)  17.9 us
    all_gather x1, blocking collectives, per_device(): group_emb = lax.all_gather(image_emb, 'branch', axis=0, tiled=True)  17.6 us
    psum x1, waiting for transfers between devices, per_device(): lax.psum((image_weight, text_weight), 'dp')  14.1 us
    reduce_scatter x1, waiting for transfers between devices, per_device(): lax.psum_scatter(normalized_exponent_divisor * jnp.dot(reduced_width_para...  14 us
  transfers between devices with their start and end apart: 5, of which 4 were waited for; matrix products, arithmetic and copies ran while one was open for 7% of the time, Pallas kernels for 0%

commit v1 on v0

--- a/solution.py
+++ b/solution.py
@@ -134,7 +134,7 @@
     )
     own_col_terms = lax.dynamic_slice_in_dim(col_lse, data_pos * own_rows, own_rows, 0)
     loss_part = (jnp.sum(own_row_terms) + jnp.sum(own_col_terms)) / denominator
-    loss_total, scale_total = lax.psum((loss_part, scale_part), ("dp", "branch"))
+    loss_total, scale_total = lax.psum(lax.psum((loss_part, scale_part), "dp"), "branch")
     return (
         loss_total.reshape(1),
         scale_total.reshape(1),

time: 284 us -> 284 us (level)
  blocking collectives: 161 us -> 146 us
  waiting for transfers between devices: 60.6 us -> 75.2 us
    psum x1 -> x2, blocking collectives: 38.5 us -> 23.4 us  [the longest x1 12.8 us: per_device(): lax.psum((loss_part, scale_part), 'dp')]
    psum x1, waiting for transfers between devices: 14.1 us -> 28.7 us  [per_device(): lax.psum((image_weight, text_weight), 'dp')]
where the time goes in v1:
time: 284 us; the launch traced here: 283 us
  blocking collectives  146 us (51%)
  waiting for transfers between devices  75.2 us (26%)
  matrix products  23.1 us (8%)
  between operations  15.9 us (6%)
  other arithmetic  12.9 us (5%)
  local copies, waits for them, and re-layouts  6.21 us (2%)
  starting transfers between devices  3.58 us (1%)
    psum x1, waiting for transfers between devices, per_device(): lax.psum((image_weight, text_weight), 'dp')  28.7 us
    reduce_scatter x1, waiting for transfers between devices, per_device(): lax.psum_scatter(normalized_exponent_divisor * lax.dot_general(reduced_wi...  25.9 us
    all_gather x1, blocking collectives, per_device(): lax.all_gather(text_down, 'branch', axis=0, tiled=True)  19.6 us
    psum x2, blocking collectives, per_device(): lax.psum((row_mass * jnp.exp(row_peak - row_highest), positive), 'branch')  19.6 us
    all_gather x1, blocking collectives, per_device(): lax.all_gather(image_down, 'branch', axis=0, tiled=True)  17.9 us
    all_gather x1, blocking collectives, per_device(): group_emb = lax.all_gather(image_emb, 'branch', axis=0, tiled=True)  17.6 us
    reduce_scatter x1, waiting for transfers between devices, per_device(): lax.psum_scatter(normalized_exponent_divisor * jnp.dot(reduced_width_para...  14 us
    all_to_all x1, blocking collectives, per_device(): lax.all_to_all(text_hidden, 'branch', split_axis=0, concat_axis=1, tiled=...  13.6 us
  transfers between devices with their start and end apart: 5, of which 4 were waited for; matrix products, arithmetic and copies ran while one was open for 7% of the time, Pallas kernels for 0%

profile of v1, /device:TPU:0, one launch (start us, length us, event | category | flops | bytes accessed | tf_op | source)
XLA Modules:
  0.0 282.5 jit_solution(16634384593390737706)
XLA Ops:
  8.3 13.6 %all_to_all.38 = bf16[4,128,192]{1,2,0:T(8,128)(2,1)S(1)} all-to-all(bf16[4,128,192]{1,2,0:T(8,128)(2,1)S(1)} %copy_bitcast_fusion), channel_id=1, replica_groups=mesh['dp'=8,'branch'=4] {'branch'}, dimensions={0} | all-to-all | bytes 393216 | tf_op jit(solution)/shard_map/all_to_all | solution.py:33
  21.9 1.7 multiply_reduce_fusion.3
  24.5 3.4 %all-to-all-start = ((bf16[4,128,256]{2,1,0:T(8,128)(2,1)}), bf16[4,128,256]{2,1,0:T(8,128)(2,1)S(1)}, u32[]{:S(2)}, u32[]{:S(2)}) async-start(bf16[4,128,256]{2,1,0:T(8,128)(2,1)} %bitcast.1), calls=%async_computation | async-start | bytes 524288 | tf_op jit(solution)/shard_map/all_to_all | solution.py:32
  29.4 6.6 %all-to-all-done = bf16[4,128,256]{2,1,0:T(8,128)(2,1)S(1)} async-done(((bf16[4,128,256]{2,1,0:T(8,128)(2,1)}), bf16[4,128,256]{2,1,0:T(8,128)(2,1)S(1)}, u32[]{:S(2)}, u32[]{:S(2)}) %all-to-all-start) | async-done | bytes 262176 | tf_op jit(solution)/shard_map/all_to_all | solution.py:32
  36.8 17.6 %all_gather.12 = bf16[512,768]{1,0:T(8,128)(2,1)S(1)} all-gather(bf16[128,768]{1,0:T(8,128)(2,1)S(1)} %fusion.19), channel_id=1, replica_groups=mesh['dp'=8,'branch'=4] {'branch'}, dimensions={0}, use_global_device_ids=true | all-gather | bytes 983040 | tf_op jit(solution)/shard_map/all_gather | solution.py:43
  54.4 3.8 %fusion.23 = (f32[1024]{0:T(1024)S(1)}, f32[512]{0:T(512)S(1)}, f32[512,1024]{1,0:T(8,128)}) fusion(bf16[512,768]{1,0:T(8,128)(2,1)S(1)} %all_gather.12, bf16[1024,768]{1,0:T(8,128)(2,1)} %all-gather.2.cloned.1.call-done, f32[]{:T(128)} %bitcast), kind=kOutput, calls=%fused_computation.55 | convolution fusion | flops 806877696 | bytes 4462596 | tf_op jit(solution)/shard_map/dot_general | solution.py:53
  58.2 10.3 %pmax.14 = f32[512]{0:T(512)S(1)} all-reduce(f32[512]{0:T(512)S(1)} %get-tuple-element.35), channel_id=1, replica_groups=mesh['dp'=8,'branch'=4] {'branch'}, use_global_device_ids=true, to_apply=%region_3.4 | all-reduce | flops 512 | bytes 4096 | tf_op jit(solution)/shard_map/pmax | solution.py:77
  68.5 11.8 %pmax.15 = f32[1024]{0:T(1024)S(1)} all-reduce(f32[1024]{0:T(1024)S(1)} %get-tuple-element.34), channel_id=1, replica_groups=mesh['dp'=8,'branch'=4] {'dp'}, use_global_device_ids=true, to_apply=%region_10.11 | all-reduce | flops 1024 | bytes 8192 | tf_op jit(solution)/shard_map/pmax | solution.py:80
  80.3 2.3 exponential_reduce_fusion
  82.7 11.9 %psum.65 = f32[1024]{0:T(1024)S(1)} all-reduce(f32[1024]{0:T(1024)S(1)} %exponential_multiply_fusion), channel_id=1, replica_groups=mesh['dp'=8,'branch'=4] {'dp'}, use_global_device_ids=true, to_apply=%region_12.13 | all-reduce | flops 1024 | bytes 8192 | tf_op jit(solution)/shard_map/psum | solution.py:81
  94.6 8.4 %psum.63 = f32[512]{0:T(512)S(1)} all-reduce(f32[512]{0:T(512)S(1)} %exponential_multiply_fusion.1), channel_id=1, replica_groups=mesh['dp'=8,'branch'=4] {'branch'}, use_global_device_ids=true, to_apply=%region_5.6 | all-reduce | flops 512 | bytes 4096 | tf_op jit(solution)/shard_map/psum | solution.py:78
  103.0 4.8 %convolution_multiply_fusion.2 = f32[512,768]{1,0:T(8,128)} fusion(bf16[1024,768]{1,0:T(8,128)(2,1)} %all-gather.2.cloned.1.call-done, f32[]{:T(128)} %bitcast, f32[512,1024]{1,0:T(8,128)} %get-tuple-element.46, f32[1024]{0:T(1024)S(1)} %log_add_fusion, f32[512]{0:T(512)S(1)} %log_add_fusion.1, s32[1024]{0:T(1024)S(1)} %fusion.15, s32[512]{0:T(512)S(1)} %dynamic_slice.15), kind=kOutput, calls=%fused_computation.11 | convolution fusion | flops 809893888 | bytes 5255172 | tf_op jit(solution)/shard_map/dot_general | solution.py:96
  107.9 4.8 %convolution_multiply_fusion = f32[1024,768]{1,0:T(8,128)} fusion(bf16[512,768]{1,0:T(8,128)(2,1)S(1)} %all_gather.12, f32[]{:T(128)} %bitcast, f32[512,1024]{1,0:T(8,128)} %get-tuple-element.46, f32[1024]{0:T(1024)S(1)} %log_add_fusion, f32[512]{0:T(512)S(1)} %log_add_fusion.1, s32[1024]{0:T(1024)S(1)} %fusion.15, s32[512]{0:T(512)S(1)} %dynamic_slice.15), kind=kOutput, calls=%fused_computation.9 | convolution fusion | flops 810287104 | bytes 6041604 | tf_op jit(solution)/shard_map/dot_general | solution.py:103
  113.5 3.6 %multiply_reduce_fusion = (f32[]{:T(128)}, f32[512]{0:T(512)S(1)}) fusion(f32[512,1024]{1,0:T(8,128)} %get-tuple-element.46, f32[1024]{0:T(1024)S(1)} %log_add_fusion, f32[512]{0:T(512)S(1)} %log_add_fusion.1, s32[1024]{0:T(1024)S(1)} %fusion.15, s32[512]{0:T(512)S(1)} %dynamic_slice.15), kind=kLoop, calls=%fused_computation.5 | loop fusion | flops 5766655 | bytes 2111492 | tf_op jit(solution)/shard_map/reduce_sum | solution.py:92
  117.1 11.2 %psum.64 = f32[512]{0:T(512)S(1)} all-reduce(f32[512]{0:T(512)S(1)} %get-tuple-element.31), channel_id=1, replica_groups=mesh['dp'=8,'branch'=4] {'branch'}, use_global_device_ids=true, to_apply=%region_7.8 | all-reduce | flops 512 | bytes 4096 | tf_op jit(solution)/shard_map/psum | solution.py:78
  128.3 14.0 %reduce-scatter.3.cloned.1.call-done = f32[128,768]{1,0:T(8,128)} async-done(((f32[512,768]{1,0:T(8,128)}), f32[128,768]{1,0:T(8,128)}) %reduce-scatter.3.cloned.1.call-update) | async-done | bytes 393232 | tf_op jit(solution)/shard_map/reduce_scatter | solution.py:94
  142.3 1.2 multiply_reduce_fusion.2
  143.5 1.1 divide_convert_fusion.1
  144.6 17.9 %all_gather.14 = bf16[512,768]{1,0:T(8,128)(2,1)S(1)} all-gather(bf16[128,768]{1,0:T(8,128)(2,1)S(1)} %divide_convert_fusion.1), channel_id=1, replica_groups=mesh['dp'=8,'branch'=4] {'branch'}, dimensions={0}, use_global_device_ids=true | all-gather | bytes 983040 | tf_op jit(solution)/shard_map/all_gather | solution.py:116
  162.5 2.2 convolution_bitcast_fusion
  164.8 25.9 %reduce-scatter.5.cloned.1.call-done = f32[128,768]{1,0:T(8,128)} async-done(((f32[1024,768]{1,0:T(8,128)}), f32[128,768]{1,0:T(8,128)}) %reduce-scatter.5.cloned.1.call-update) | async-done | bytes 393232 | tf_op jit(solution)/shard_map/reduce_scatter | solution.py:101
  190.7 1.2 multiply_reduce_fusion.1
  191.8 1.1 divide_convert_fusion
  193.0 19.6 %all_gather.15 = bf16[512,768]{1,0:T(8,128)(2,1)S(1)} all-gather(bf16[128,768]{1,0:T(8,128)(2,1)S(1)} %divide_convert_fusion), channel_id=1, replica_groups=mesh['dp'=8,'branch'=4] {'branch'}, dimensions={0}, use_global_device_ids=true | all-gather | bytes 983040 | tf_op jit(solution)/shard_map/all_gather | solution.py:117
  212.5 2.1 convolution_bitcast_fusion.1
  216.6 12.8 %all-reduce = (f32[]{:T(128)}, f32[]{:T(128)}) all-reduce(f32[]{:T(128)S(6)} %div.53, f32[]{:T(128)} %get-tuple-element.30), channel_id=1, replica_groups=mesh['dp'=8,'branch'=4] {'dp'}, use_global_device_ids=true, to_apply=%region_14.15 | all-reduce | flops 2 | bytes 16 | tf_op jit(solution)/shard_map/psum | solution.py:137
  229.4 10.6 %all-reduce.2 = (f32[1]{0:T(128)}, f32[1]{0:T(128)}) all-reduce(f32[1]{0:T(128)} %bitcast.6, f32[1]{0:T(128)} %bitcast.7), channel_id=1, replica_groups=mesh['dp'=8,'branch'=4] {'branch'}, use_global_device_ids=true, to_apply=%region_15.16 | all-reduce | flops 2 | bytes 16 | tf_op jit(solution)/shard_map/psum | solution.py:137
  240.0 1.1 convolution_convert_fusion
  241.1 2.0 convolution_convert_fusion.1
  243.2 28.7 %all-reduce.5.cloned.1.call-done = (f32[256,768]{0,1:T(8,128)}, f32[192,768]{1,0:T(8,128)}) async-done(((f32[256,768]{0,1:T(8,128)}, f32[192,768]{1,0:T(8,128)}), (f32[256,768]{0,1:T(8,128)}, f32[192,768]{1,0:T(8,128)})) %all-reduce.5.cloned.1.call-update) | async-done | bytes 1376272 | tf_op jit(solution)/shard_map/psum | solution.py:131
  271.8 2.3 copy.19
  274.1 1.9 copy.25
  (27 shorter events, 5.0 us)
Async XLA Ops:
  7.2 29.0 %copy-start = (bf16[1024,768]{1,0:T(8,128)(2,1)S(1)}, bf16[1024,768]{1,0:T(8,128)(2,1)}, u32[]{:S(2)}) copy-start(bf16[1024,768]{1,0:T(8,128)(2,1)} %param.8) | copy-start | bytes 4718596
  7.2 47.2 %all-gather.2.cloned.1.call-start = ((), (), s32[]{:S(2)}) async-start(), calls=%async_computation.4 | async-start | bytes 1769472 | tf_op jit(solution)/shard_map/all_gather | solution.py:49
  24.5 11.6 %all-to-all-start = ((bf16[4,128,256]{2,1,0:T(8,128)(2,1)}), bf16[4,128,256]{2,1,0:T(8,128)(2,1)S(1)}, u32[]{:S(2)}, u32[]{:S(2)}) async-start(bf16[4,128,256]{2,1,0:T(8,128)(2,1)} %bitcast.1), calls=%async_computation | async-start | bytes 524288 | tf_op jit(solution)/shard_map/all_to_all | solution.py:32
  27.9 114.4 %reduce-scatter.3.cloned.1.call-start = ((), (), s32[]{:S(2)}) async-start(), calls=%async_computation.5 | async-start | bytes 1966080 | tf_op jit(solution)/shard_map/reduce_scatter | solution.py:94
  107.8 82.8 %reduce-scatter.5.cloned.1.call-start = ((), (), s32[]{:S(2)}) async-start(), calls=%async_computation.6 | async-start | bytes 3538944 | tf_op jit(solution)/shard_map/reduce_scatter | solution.py:101
  112.8 159.1 %all-reduce.5.cloned.1.call-start = ((), (), s32[]{:S(2)}) async-start(), calls=%async_computation.7 | async-start | bytes 2752512 | tf_op jit(solution)/shard_map/psum | solution.py:131
Sparse Core Ops, SparseCore 0:
  24.6 24.6 all-gather.1
  108.0 34.2 reduce-scatter.2
  145.7 44.9 reduce-scatter.4
  214.8 57.0 all-reduce.4
